TPU v7x, 8 devices: a whole 2x2x1 slice. The times are simulated.
8 devices in a mesh: rep: 2 (over y, z), dp: 4 (over x, core).
Axes of the slice: x: 2, y: 2, z: 1, core: 2. Of those that a mesh axis runs over, the one named last changes fastest.
Arguments:
- x: bfloat16 [8, 2048, 1024], P(('rep', 'dp')), parts along dimension 0
- dy: bfloat16 [8, 2048, 1024], P(('rep', 'dp')), parts along dimension 0
- w_gate: bfloat16 [2, 1024, 2816], replicated
- w_up: bfloat16 [2, 1024, 2816], replicated
- w_down: bfloat16 [2, 2816, 1024], replicated
- m_w_gate: float32 [2, 1024, 2816], P(None, 'dp')
- m_w_up: float32 [2, 1024, 2816], P(None, 'dp')
- m_w_down: float32 [2, 2816, 1024], P(None, 'dp')
- v_w_gate: float32 [2, 1024, 2816], P(None, 'dp')
- v_w_up: float32 [2, 1024, 2816], P(None, 'dp')
- v_w_down: float32 [2, 2816, 1024], P(None, 'dp')
Outputs:
- output 1: bfloat16 [4, 1024, 2816], P('rep'), parts along dimension 0
- output 2: bfloat16 [4, 1024, 2816], P('rep'), parts along dimension 0
- output 3: bfloat16 [4, 2816, 1024], P('rep'), parts along dimension 0
- output 4: float32 [4, 1024, 2816], P('rep', 'dp'), parts along dimension 0
- output 5: float32 [4, 1024, 2816], P('rep', 'dp'), parts along dimension 0
- output 6: float32 [4, 2816, 1024], P('rep', 'dp'), parts along dimension 0
- output 7: float32 [4, 1024, 2816], P('rep', 'dp'), parts along dimension 0
- output 8: float32 [4, 1024, 2816], P('rep', 'dp'), parts along dimension 0
- output 9: float32 [4, 2816, 1024], P('rep', 'dp'), parts along dimension 0
There are 2 independent parts. A program takes and returns all parts, laid end to end along the dimension named above; an argument that names none is the same for every part.
All inputs are finite; a program needn't handle non-finite values.
Results may differ from a plain program's by a relative error of at most 0.022.
Values are sent between devices in bfloat16 or wider.
A program may use at most 2 GiB of HBM per device.

v0:
```python
import jax
import jax.numpy as jnp
from jax import lax

NAMES = ("w_gate", "w_up", "w_down")


def matmul(a, w):
    return jnp.dot(a, w, preferred_element_type=jnp.float32).astype(jnp.bfloat16)


def normed(h):
    wide = h.astype(jnp.float32)
    scale = lax.rsqrt(jnp.mean(wide**2, -1, keepdims=True) + 1e-6)
    return (wide * scale).astype(jnp.bfloat16)


def layer(h, w):
    a = normed(h)
    gate = jnp.dot(a, w["w_gate"], preferred_element_type=jnp.float32)
    up = jnp.dot(a, w["w_up"], preferred_element_type=jnp.float32)
    return h + matmul((jax.nn.silu(gate) * up).astype(jnp.bfloat16), w["w_down"])


def adamw(w, m, v, g):
    m = 0.9 * m + 0.1 * g
    v = 0.95 * v + 0.05 * g * g
    step = m * lax.rsqrt(v + 1e-8) + 0.1 * w
    return (w - 0.02 * step).astype(jnp.bfloat16), m, v


def clipped(gradients, sum_of_squares, count):
    factor = jnp.minimum(1.0, 0.5 * lax.rsqrt(sum_of_squares / count + 1e-30))
    return [g * factor for g in gradients]


def stack(weights, h):
    for number in range(weights["w_gate"].shape[0]):
        h = layer(h, {name: w[number] for name, w in weights.items()})
    return h


def solution(mesh):
    groups = mesh.shape["rep"]

    def step(x, dy, *arrays):
        weights, m, v = (arrays[i : i + 3] for i in (0, 3, 6))
        x, dy = (t.reshape(groups, -1, *t.shape[1:]) for t in (x, dy))

        def of_a_group(x, dy):
            _, back = jax.vjp(lambda w: stack(w, x), dict(zip(NAMES, weights, strict=True)))
            by_weights = back(dy)[0]
            gradients = [by_weights[name].astype(jnp.float32) for name in NAMES]
            gradients = clipped(gradients, sum(jnp.sum(g * g) for g in gradients), sum(g.size for g in gradients))
            new = [adamw(w.astype(jnp.float32), m, v, g) for w, m, v, g in zip(weights, m, v, gradients, strict=True)]
            return tuple(one[which] for which in range(3) for one in new)

        return tuple(t.reshape(-1, *t.shape[2:]) for t in jax.vmap(of_a_group)(x, dy))

    return step
```

profile of v0, /device:TPU:0, one launch (start us, length us, event | category | flops | bytes accessed | tf_op | source)
XLA Modules:
  0.0 999.6 jit_solution(17395327745163430892)
XLA Ops:
  16.8 20.0 %fusion.94 = f32[2048,2816]{1,0:T(8,128)} fusion(bf16[2,1024,2816]{2,1,0:T(8,128)(2,1)} %param, bf16[1,2048,1024]{2,1,0:T(8,128)(2,1)} %param.2, f32[2048]{0:T(1024)S(1)} %add_rsqrt_fusion), kind=kOutput, calls=%fused_computation.121 | convolution fusion | flops 11817451520 | bytes 33038336 | tf_op jit(solution)/vmap(jvp())/dot_general | solution.py:20
  36.8 18.2 %fusion.92 = f32[2048,2816]{1,0:T(8,128)} fusion(bf16[2,1024,2816]{2,1,0:T(8,128)(2,1)} %param.3, bf16[1,2048,1024]{2,1,0:T(8,128)(2,1)S(1)} %copy-done.1, f32[2048]{0:T(1024)S(1)} %add_rsqrt_fusion), kind=kOutput, calls=%fused_computation.119 | convolution fusion | flops 11817451520 | bytes 33038336 | tf_op jit(solution)/vmap(jvp())/dot_general | solution.py:21
  54.9 19.6 %fusion.26 = bf16[2048,2816]{1,0:T(8,128)(2,1)} fusion(f32[2048,2816]{1,0:T(8,128)} %fusion.92, f32[2048,2816]{1,0:T(8,128)} %fusion.94), kind=kLoop, calls=%fused_computation.39 | loop fusion | flops 34603008 | bytes 57671680
  74.6 19.4 %fusion.39 = (f32[2048]{0:T(1024)S(1)}, bf16[1,1,2048,1024]{2,3,1,0:T(8,128)(2,1)}) fusion(bf16[2048,2816]{1,0:T(8,128)(2,1)} %fusion.26, bf16[2,2816,1024]{2,1,0:T(8,128)(2,1)} %param.4, bf16[1,2048,1024]{1,2,0:T(8,128)(2,1)} %copy), kind=kOutput, calls=%fused_computation.59 | convolution fusion | flops 11821643776 | bytes 25698304 | tf_op jit(solution)/vmap(jvp())/dot_general | solution.py:9
  94.6 20.2 %fusion.81 = f32[2048,2816]{1,0:T(8,128)} fusion(bf16[2,1024,2816]{2,1,0:T(8,128)(2,1)} %param, bf16[1,1,2048,1024]{2,3,1,0:T(8,128)(2,1)} %get-tuple-element.10, f32[2048]{0:T(1024)S(1)} %bitcast.339), kind=kOutput, calls=%fused_computation.108 | convolution fusion | flops 11817451520 | bytes 33038336 | tf_op jit(solution)/vmap(jvp())/dot_general | solution.py:20
  114.8 18.2 %fusion.85 = f32[2048,2816]{1,0:T(8,128)} fusion(bf16[2,1024,2816]{2,1,0:T(8,128)(2,1)} %param.3, bf16[1,1,2048,1024]{2,3,1,0:T(8,128)(2,1)S(1)} %copy-done.7, f32[2048]{0:T(1024)S(1)} %bitcast.340), kind=kOutput, calls=%fused_computation.112 | convolution fusion | flops 11817451520 | bytes 33038336 | tf_op jit(solution)/vmap(jvp())/dot_general | solution.py:21
  133.1 24.2 %fusion.51 = f32[1,2816,1024]{2,1,0:T(8,128)} fusion(f32[2048,2816]{1,0:T(8,128)} %fusion.85, f32[2048,2816]{1,0:T(8,128)} %fusion.81, bf16[1,2048,1024]{2,1,0:T(8,128)(2,1)S(1)} %copy-done.10), kind=kOutput, calls=%fused_computation.80 | convolution fusion | flops 11845763072 | bytes 61865984 | tf_op jit(solution)/vmap(transpose(jvp()))/dot_general | solution.py:9
  164.4 20.2 %convolution_convert_fusion.1 = bf16[2048,2816]{1,0:T(8,128)(2,1)} fusion(bf16[2,2816,1024]{2,1,0:T(8,128)(2,1)} %param.4, bf16[1,2048,1024]{2,1,0:T(8,128)(2,1)} %param.5), kind=kOutput, calls=%fused_computation.48 | convolution fusion | flops 11816927232 | bytes 21495808 | tf_op jit(solution)/vmap(transpose(jvp()))/dot_general | solution.py:9
  184.5 24.0 %fusion.6 = bf16[2048,2816]{1,0:T(8,128)(2,1)} fusion(f32[2048,2816]{1,0:T(8,128)} %fusion.81, f32[2048,2816]{1,0:T(8,128)} %fusion.85, bf16[2048,2816]{1,0:T(8,128)(2,1)} %convolution_convert_fusion.1), kind=kLoop, calls=%fused_computation.11 | loop fusion | flops 69206016 | bytes 69206016
  210.5 20.6 %fusion.24 = bf16[2048,1024]{0,1:T(8,128)(2,1)} fusion(bf16[2048,2816]{1,0:T(8,128)(2,1)S(1)} %copy-done.6, f32[2048,2816]{1,0:T(8,128)} %fusion.81, bf16[2,1024,2816]{2,1,0:T(8,128)(2,1)} %param.3), kind=kOutput, calls=%fused_computation.34 | convolution fusion | flops 11845763072 | bytes 44564480 | tf_op jit(solution)/vmap(transpose(jvp()))/dot_general | solution.py:21
  231.1 20.3 %fusion.41 = (f32[2048]{0:T(1024)S(1)}, bf16[2048,1024]{0,1:T(8,128)(2,1)}) fusion(bf16[1,1,2048,1024]{2,3,1,0:T(8,128)(2,1)} %get-tuple-element.10, bf16[2048,1024]{0,1:T(8,128)(2,1)} %fusion.24, bf16[2048,2816]{1,0:T(8,128)(2,1)} %fusion.6, bf16[2,1024,2816]{2,1,0:T(8,128)(2,1)} %param), kind=kOutput, calls=%fused_computation.61 | convolution fusion | flops 11821643776 | bytes 29892608 | tf_op jit(solution)/vmap(transpose(jvp()))/dot_general | solution.py:20
  258.3 17.7 %convolution_bitcast_fusion = f32[1,2816,1024]{2,1,0:T(8,128)} fusion(bf16[2048,2816]{1,0:T(8,128)(2,1)} %fusion.26, bf16[2048,1024]{0,1:T(8,128)(2,1)S(1)} %fusion.108), kind=kOutput, calls=%fused_computation.81 | convolution fusion | flops 11811160064 | bytes 27262976 | tf_op jit(solution)/vmap(transpose(jvp()))/dot_general | solution.py:9
  276.0 27.9 %fusion.45 = f32[1,1024,2816]{2,1,0:T(8,128)} fusion(bf16[2048,2816]{1,0:T(8,128)(2,1)} %convolution_convert_fusion.1, f32[2048,2816]{1,0:T(8,128)} %fusion.81, bf16[1,1,2048,1024]{2,3,1,0:T(8,128)(2,1)} %get-tuple-element.10, f32[2048]{0:T(1024)S(1)} %bitcast.342), kind=kOutput, calls=%fused_computation.78 | convolution fusion | flops 11852054528 | bytes 50339840 | tf_op jit(solution)/vmap(transpose(jvp()))/dot_general | solution.py:21
  304.0 18.2 %convolution_convert_fusion = bf16[2048,2816]{1,0:T(8,128)(2,1)} fusion(bf16[2048,1024]{0,1:T(8,128)(2,1)} %copy-done.9, bf16[2,2816,1024]{2,1,0:T(8,128)(2,1)} %param.4), kind=kOutput, calls=%fused_computation.47 | convolution fusion | flops 11816927232 | bytes 21495808 | tf_op jit(solution)/vmap(transpose(jvp()))/dot_general | solution.py:9
  322.2 24.0 %fusion.48 = f32[1,1024,2816]{2,1,0:T(8,128)} fusion(bf16[2048,2816]{1,0:T(8,128)(2,1)} %convolution_convert_fusion, f32[2048,2816]{1,0:T(8,128)} %fusion.94, bf16[1,2048,1024]{1,2,0:T(8,128)(2,1)} %copy, f32[2048]{0:T(1024)S(1)} %copy-done.16), kind=kOutput, calls=%fused_computation.79 | convolution fusion | flops 11852054528 | bytes 50339840 | tf_op jit(solution)/vmap(transpose(jvp()))/dot_general | solution.py:21
  346.3 18.7 %convolution_bitcast_fusion.1 = f32[1,1024,2816]{2,1,0:T(8,128)} fusion(bf16[2048,2816]{1,0:T(8,128)(2,1)} %fusion.6, bf16[1,1,2048,1024]{2,3,1,0:T(8,128)(2,1)} %get-tuple-element.10, f32[2048]{0:T(1024)S(1)} %bitcast.343), kind=kOutput, calls=%fused_computation.82 | convolution fusion | flops 11817451520 | bytes 27271168 | tf_op jit(solution)/vmap(transpose(jvp()))/dot_general | solution.py:20
  365.0 32.5 %fusion.54 = f32[1,1024,2816]{2,1,0:T(8,128)} fusion(f32[2048,2816]{1,0:T(8,128)} %fusion.94, f32[2048,2816]{1,0:T(8,128)} %fusion.92, bf16[2048,2816]{1,0:T(8,128)(2,1)} %convolution_convert_fusion, bf16[1,2048,1024]{1,2,0:T(8,128)(2,1)} %copy, f32[2048]{0:T(1024)S(1)} %copy-done.16), kind=kOutput, calls=%fused_computation.83 | convolution fusion | flops 11880890368 | bytes 73408512 | tf_op jit(solution)/vmap(transpose(jvp()))/dot_general | solution.py:20
  407.3 45.9 %reduce-scatter.23.cloned.1.call-done = f32[1,256,2816]{2,1,0:T(8,128)} async-done(((f32[1,1024,2816]{2,1,0:T(8,128)}), f32[1,256,2816]{2,1,0:T(8,128)}) %reduce-scatter.23.cloned.1.call-update) | async-done | bytes 2883600
  455.2 85.8 %reduce-scatter.25.cloned.1.call-done = f32[1,256,2816]{2,1,0:T(8,128)} async-done(((f32[1,1024,2816]{2,1,0:T(8,128)}), f32[1,256,2816]{2,1,0:T(8,128)}) %reduce-scatter.25.cloned.1.call-update) | async-done | bytes 2883600
  545.0 83.7 %reduce-scatter.19.cloned.1.call-done = f32[1,256,2816]{2,1,0:T(8,128)} async-done(((f32[1,1024,2816]{2,1,0:T(8,128)}), f32[1,256,2816]{2,1,0:T(8,128)}) %reduce-scatter.19.cloned.1.call-update) | async-done | bytes 2883600
  631.8 85.3 %reduce-scatter.21.cloned.1.call-done = f32[1,256,2816]{2,1,0:T(8,128)} async-done(((f32[1,1024,2816]{2,1,0:T(8,128)}), f32[1,256,2816]{2,1,0:T(8,128)}) %reduce-scatter.21.cloned.1.call-update) | async-done | bytes 2883600
  767.8 50.1 %all-gather.14.cloned.1.call-done = bf16[1,2,2816,1024]{3,2,1,0:T(8,128)(2,1)} async-done(((bf16[1,2,704,1024]{3,2,1,0:T(8,128)(2,1)}), bf16[1,2,2816,1024]{3,2,1,0:T(8,128)(2,1)}) %all-gather.14.cloned.1.call-update) | async-done | bytes 11534352 | tf_op jit(solution)/reshape | solution.py:58
  817.9 75.5 %all-gather.10.cloned.1.call-done = bf16[1,2,1024,2816]{3,2,1,0:T(8,128)(2,1)} async-done(((bf16[1,2,256,2816]{3,2,1,0:T(8,128)(2,1)}), bf16[1,2,1024,2816]{3,2,1,0:T(8,128)(2,1)}) %all-gather.10.cloned.1.call-update) | async-done | bytes 11534352 | tf_op jit(solution)/reshape | solution.py:58
  893.4 75.5 %all-gather.12.cloned.1.call-done = bf16[1,2,1024,2816]{3,2,1,0:T(8,128)(2,1)} async-done(((bf16[1,2,256,2816]{3,2,1,0:T(8,128)(2,1)}), bf16[1,2,1024,2816]{3,2,1,0:T(8,128)(2,1)}) %all-gather.12.cloned.1.call-update) | async-done | bytes 11534352 | tf_op jit(solution)/reshape | solution.py:58
  (88 shorter events, 116.2 us)
Async XLA Ops:
  7.2 392.3 %reduce-scatter.27.cloned.1.call-start = ((), (), s32[]{:S(2)}) async-start(), calls=%async_computation.13 | async-start | bytes 14417920
  16.7 20.0 %copy-start.15 = (f32[2048]{0:T(1024)}, f32[2048]{0:T(1024)S(1)}, u32[]{:S(2)}) copy-start(f32[2048]{0:T(1024)S(1)} %add_rsqrt_fusion) | copy-start | bytes 24580
  16.7 20.0 %copy-start.1 = (bf16[1,2048,1024]{2,1,0:T(8,128)(2,1)S(1)}, bf16[1,2048,1024]{2,1,0:T(8,128)(2,1)}, u32[]{:S(2)}) copy-start(bf16[1,2048,1024]{2,1,0:T(8,128)(2,1)} %param.2) | copy-start | bytes 12582916
  94.0 20.8 %copy-start.13 = (f32[1,1,2048]{2,1,0:T(1,128)}, f32[1,1,2048]{2,1,0:T(1,128)S(1)}, u32[]{:S(2)}) copy-start(f32[1,1,2048]{2,1,0:T(1,128)S(1)} %rsqrt.38) | copy-start | bytes 24580
  94.6 20.2 %copy-start.7 = (bf16[1,1,2048,1024]{2,3,1,0:T(8,128)(2,1)S(1)}, bf16[1,1,2048,1024]{2,3,1,0:T(8,128)(2,1)}, u32[]{:S(2)}) copy-start(bf16[1,1,2048,1024]{2,3,1,0:T(8,128)(2,1)} %get-tuple-element.10) | copy-start | bytes 12582916
  114.8 18.3 %copy-start.10 = (bf16[1,2048,1024]{2,1,0:T(8,128)(2,1)S(1)}, bf16[1,2048,1024]{2,1,0:T(8,128)(2,1)}, u32[]{:S(2)}) copy-start(bf16[1,2048,1024]{2,1,0:T(8,128)(2,1)} %param.5) | copy-start | bytes 12582916
  157.3 244.3 %reduce-scatter.29.cloned.1.call-start = ((), (), s32[]{:S(2)}) async-start(), calls=%async_computation.14 | async-start | bytes 14417920
  184.5 25.9 %copy-start.6 = (bf16[2048,2816]{1,0:T(8,128)(2,1)S(1)}, bf16[2048,2816]{1,0:T(8,128)(2,1)}, u32[]{:S(2)}) copy-start(bf16[2048,2816]{1,0:T(8,128)(2,1)} %convolution_convert_fusion.1) | copy-start | bytes 34603012
  231.1 20.4 %copy-start.12 = (f32[2048]{0:T(1024)S(1)}, f32[2048]{0:T(1024)}, u32[]{:S(2)}) copy-start(f32[2048]{0:T(1024)} %copy-done.11) | copy-start | bytes 24580
  231.1 20.4 %copy-start = (bf16[1,2048,1024]{1,2,0:T(8,128)(2,1)S(1)}, bf16[1,2048,1024]{1,2,0:T(8,128)(2,1)}, u32[]{:S(2)}) copy-start(bf16[1,2048,1024]{1,2,0:T(8,128)(2,1)} %copy.1) | copy-start | bytes 12582916
  231.1 20.4 %copy-start.8 = (bf16[1,1,2048,1024]{2,3,1,0:T(8,128)(2,1)S(1)}, bf16[1,1,2048,1024]{2,3,1,0:T(8,128)(2,1)}, u32[]{:S(2)}) copy-start(bf16[1,1,2048,1024]{2,3,1,0:T(8,128)(2,1)} %get-tuple-element.10) | copy-start | bytes 12582916
  231.1 20.4 %copy-start.14 = (f32[1,1,2048]{2,1,0:T(1,128)S(1)}, f32[1,1,2048]{2,1,0:T(1,128)}, u32[]{:S(2)}) copy-start(f32[1,1,2048]{2,1,0:T(1,128)} %copy-done.13) | copy-start | bytes 24580
  276.0 177.2 %reduce-scatter.23.cloned.1.call-start = ((), (), s32[]{:S(2)}) async-start(), calls=%async_computation.11 | async-start | bytes 14417920
  303.9 18.3 %copy-start.16 = (f32[2048]{0:T(1024)S(1)}, f32[2048]{0:T(1024)}, u32[]{:S(2)}) copy-start(f32[2048]{0:T(1024)} %copy-done.15) | copy-start | bytes 24580
  303.9 237.1 %reduce-scatter.25.cloned.1.call-start = ((), (), s32[]{:S(2)}) async-start(), calls=%async_computation.12 | async-start | bytes 14417920
  346.2 282.6 %reduce-scatter.19.cloned.1.call-start = ((), (), s32[]{:S(2)}) async-start(), calls=%async_computation.9 | async-start | bytes 14417920
  365.0 352.1 %reduce-scatter.21.cloned.1.call-start = ((), (), s32[]{:S(2)}) async-start(), calls=%async_computation.10 | async-start | bytes 14417920
  397.5 420.4 %all-gather.14.cloned.1.call-start = ((), (), s32[]{:S(2)}) async-start(), calls=%async_computation.8 | async-start | bytes 14417920 | tf_op jit(solution)/reshape | solution.py:58
  743.8 149.6 %all-gather.10.cloned.1.call-start = ((), (), s32[]{:S(2)}) async-start(), calls=%async_computation.6 | async-start | bytes 14417920 | tf_op jit(solution)/reshape | solution.py:58
  757.8 211.1 %all-gather.12.cloned.1.call-start = ((), (), s32[]{:S(2)}) async-start(), calls=%async_computation.7 | async-start | bytes 14417920 | tf_op jit(solution)/reshape | solution.py:58
  968.9 11.7 %copy-start.5 = (bf16[1,2,1024,2816]{3,2,1,0:T(8,128)(2,1)S(1)}, bf16[1,2,1024,2816]{3,2,1,0:T(8,128)(2,1)}, u32[]{:S(2)}) copy-start(bf16[1,2,1024,2816]{3,2,1,0:T(8,128)(2,1)} %all-gather.12.cloned.1.call-done) | copy-start | bytes 34603012
  968.9 17.5 %slice-start = ((s8[11534336]{0:T(1024)(128)(4,1)}), s8[4194304]{0:T(1024)(128)(4,1)S(1)}, s32[]{:S(2)}) async-start(s8[11534336]{0:T(1024)(128)(4,1)} %bitcast.331), calls=%async_computation.15 | async-start | bytes 8388608
  968.9 18.3 %slice-start.1 = ((s8[11534336]{0:T(1024)(128)(4,1)}), s8[4194304]{0:T(1024)(128)(4,1)S(1)}, s32[]{:S(2)}) async-start(s8[11534336]{0:T(1024)(128)(4,1)} %bitcast.331), calls=%async_computation.16 | async-start | bytes 8388608
  980.6 7.9 slice-start.2
  (6 other events, 11.2 us)
Sparse Core Ops, SparseCore 0:
  157.4 88.1 reduce-scatter.26
  276.1 89.1 reduce-scatter.28
  367.8 85.3 reduce-scatter.22
  455.6 85.3 reduce-scatter.24
  543.4 85.3 reduce-scatter.18
  631.7 85.3 reduce-scatter.20
  743.9 73.9 all-gather.13
  820.0 73.3 all-gather.9
  895.5 73.3 all-gather.11
where the time goes:
time: 1010 us; the launch traced here: 1000 us
  waiting for transfers between devices  502 us (50%)
  matrix products  320 us (32%)
  other arithmetic  107 us (11%)
  local copies, waits for them, and re-layouts  45.3 us (4%)
  between operations  17.6 us (2%)
    unnamed x15, waiting for transfers between devices  301 us
    reshape x3, waiting for transfers between devices, step(): t.reshape(-1, *t.shape[2:])  201 us
    dot_general x5, matrix products, layer(): gate = jnp.dot(a, w['w_gate'], preferred_element_type=jnp.float32)  112 us
    dot_general x5, matrix products, layer(): up = jnp.dot(a, w['w_up'], preferred_element_type=jnp.float32)  109 us
    dot_general x5, matrix products, matmul(): jnp.dot(a, w, preferred_element_type=jnp.float32).astype(jnp.bfloat16)  99.7 us
    unnamed x4, other arithmetic  48.4 us
    unnamed x47, local copies, waits for them, and re-layouts  44.7 us
    reshape x3, other arithmetic, step(): t.reshape(-1, *t.shape[2:])  34.4 us
  transfers between devices with their start and end apart: 9, of which 7 were waited for; matrix products, arithmetic and copies ran while one was open for 28% of the time, Pallas kernels for 0%

commit v1 on v0

v1 whole, which is shorter than its diff:
```python
import functools

import jax
import jax.numpy as jnp
from jax import lax
from jax.experimental import pallas as pl
from jax.experimental.pallas import tpu as pltpu
from jax.sharding import PartitionSpec as P


F32, BF16 = jnp.float32, jnp.bfloat16
T, D, FF, DP, CORES = 2048, 1024, 2816, 4, 2
COUNT = 3 * 2 * D * FF
CHUNK = 256
CHUNKS = FF // CHUNK
ROWS = 512
VMEM_LIMIT = 62 * 2**20
ANY = pl.BlockSpec(memory_space=pl.ANY)


def dot(a, b):
    return lax.dot_general(a, b, (((1,), (0,)), ((), ())), preferred_element_type=F32)


def dot_t(a, b):
    return lax.dot_general(a, b, (((1,), (1,)), ((), ())), preferred_element_type=F32)


def whole(shape):
    return pl.BlockSpec(shape, lambda *_: (0,) * len(shape), pipeline_mode=pl.Buffered(1))


def params():
    return pltpu.CompilerParams(vmem_limit_bytes=VMEM_LIMIT, dimension_semantics=("arbitrary",))


def cost(matmuls, moved):
    return pl.CostEstimate(flops=int(2 * T * D * FF * matmuls), bytes_accessed=int(moved), transcendentals=0)


def root_mean_scale(wide):
    return lax.rsqrt(jnp.mean(wide * wide, -1, keepdims=True) + 1e-6)


def forward_first(x, w_gate, w_up, w_down):
    def kernel(x_ref, wg_ref, wu_ref, wd_ref, g_ref, u_ref, a_ref, h_ref, n_ref, acc):
        j = pl.program_id(0)

        @pl.when(j == 0)
        def _():
            for t in range(0, T, ROWS):
                rows = slice(t, t + ROWS)
                wide = x_ref[rows].astype(F32)
                a_ref[rows] = (wide * root_mean_scale(wide)).astype(BF16)
                acc[rows] = jnp.zeros((ROWS, D), F32)

        for t in range(0, T, ROWS):
            rows = slice(t, t + ROWS)
            a = a_ref[rows]
            g = dot(a, wg_ref[...])
            u = dot(a, wu_ref[...])
            g_ref[rows] = g
            u_ref[rows] = u
            act = (g * jax.nn.sigmoid(g) * u).astype(BF16)
            acc[rows] += dot(act, wd_ref[...])

        @pl.when(j == CHUNKS - 1)
        def _():
            for t in range(0, T, ROWS):
                rows = slice(t, t + ROWS)
                h = x_ref[rows] + acc[rows].astype(BF16)
                h_ref[rows] = h
                wide = h.astype(F32)
                n_ref[rows] = (wide * root_mean_scale(wide)).astype(BF16)

    tall = jax.ShapeDtypeStruct((T, FF), F32)
    flat = jax.ShapeDtypeStruct((T, D), BF16)
    wide_block = pl.BlockSpec((T, CHUNK), lambda j: (0, j))
    return pl.pallas_call(
        kernel,
        grid=(CHUNKS,),
        in_specs=[
            whole((T, D)),
            pl.BlockSpec((None, D, CHUNK), lambda j: (0, 0, j)),
            pl.BlockSpec((None, D, CHUNK), lambda j: (0, 0, j)),
            pl.BlockSpec((None, CHUNK, D), lambda j: (0, j, 0)),
        ],
        out_specs=[wide_block, wide_block, whole((T, D)), whole((T, D)), whole((T, D))],
        out_shape=[tall, tall, flat, flat, flat],
        scratch_shapes=[pltpu.VMEM((T, D), F32)],
        compiler_params=params(),
        cost_estimate=cost(3, 90e6),
    )(x, w_gate, w_up, w_down)


def hidden(layer, first, count, order, normed, by_out, weights, gate_up, chain, after):
    w_gate, w_up, w_down = weights
    computed = gate_up is None
    n_chain = len(chain)
    n_after = len(after)

    def kernel(order_ref, n_ref, by_ref, wd_ref, a_ref, b_ref, *rest):
        rest = rest[n_chain + n_after :]
        if computed:
            send_ref, keep_ref, act_ref, dg_ref, du_ref, n_t, act = rest
        else:
            send_ref, keep_ref, act_ref, n_t, act, dg_ref, du_ref = rest

        @pl.when(pl.program_id(0) == 0)
        def _():
            for k in range(DP):
                columns = pl.ds(pl.multiple_of(order_ref[k] * (D // DP), D // DP), D // DP)
                n_t[k * (D // DP) : (k + 1) * (D // DP)] = n_ref[:, columns].T

        for t in range(0, T, ROWS):
            rows = slice(t, t + ROWS)
            if computed:
                n = n_ref[rows]
                g, u = dot(n, a_ref[...]), dot(n, b_ref[...])
            else:
                g, u = a_ref[rows], b_ref[rows]
            p = dot_t(by_ref[rows], wd_ref[...]).astype(BF16).astype(F32)
            sig = jax.nn.sigmoid(g)
            silu = g * sig
            act[rows] = (silu * u).astype(BF16)
            du_ref[rows] = (p * silu).astype(BF16)
            dg_ref[rows] = (p * u * (sig + silu * (1.0 - sig))).astype(BF16)
        act_ref[...] = act[...].T
        for which, d_ref in ((0, dg_ref), (1, du_ref)):
            d = d_ref[...]
            half = D // CORES
            out = dot(n_t[:half], d).astype(BF16)
            send_ref[which] = out.reshape(CORES, half // CORES, CHUNK)
            out = dot(n_t[half:], d).astype(BF16)
            keep_ref[which] = out.reshape(CORES, half // CORES, CHUNK)

    column = pl.BlockSpec((None, D, CHUNK), lambda j, _: (layer, 0, first + j))
    block = pl.BlockSpec((T, CHUNK), lambda j, _: (0, first + j))
    part = pl.BlockSpec((2, CORES, D // DP, CHUNK), lambda j, _: (0, 0, 0, j))
    part_shape = jax.ShapeDtypeStruct((2, CORES, D // DP, count * CHUNK), BF16)
    turned = pl.BlockSpec((CHUNK, T), lambda j, _: (first + j, 0))
    turned_shape = jax.ShapeDtypeStruct((FF, T), BF16)
    out_specs, out_shape = [part, part, turned], [part_shape, part_shape, turned_shape]
    scratch = [pltpu.VMEM((D, T), BF16), pltpu.VMEM((T, CHUNK), BF16)]
    if computed:
        out_specs += [block, block]
        out_shape += [jax.ShapeDtypeStruct((T, FF), BF16)] * 2
    else:
        scratch += [pltpu.VMEM((T, CHUNK), BF16)] * 2
    return pl.pallas_call(
        kernel,
        grid_spec=pltpu.PrefetchScalarGridSpec(
            num_scalar_prefetch=1,
            grid=(count,),
            in_specs=[
                whole((T, D)),
                whole((T, D)),
                pl.BlockSpec((None, CHUNK, D), lambda j, _: (layer, first + j, 0)),
                *((column, column) if computed else (block, block)),
                *(ANY,) * (n_chain + n_after),
            ],
            out_specs=out_specs,
            scratch_shapes=scratch,
        ),
        out_shape=out_shape,
        input_output_aliases={6 + i: 2 + i for i in range(n_chain)},
        compiler_params=params(),
        cost_estimate=cost((5 if computed else 3) * count / CHUNKS, 60e6 * count / CHUNKS),
    )(order, normed, by_out, w_down, *((w_gate, w_up) if computed else gate_up), *chain, *after)


def down_grad(order, act_t, by_out, first, count, after):
    n_after = len(after)

    def kernel(order_ref, send_act, keep_act, by_ref, *rest):
        send_ref, keep_ref = rest[n_after:]
        send_ref[...] = dot(send_act[...], by_ref[...]).astype(BF16)
        keep_ref[...] = dot(keep_act[...], by_ref[...]).astype(BF16)

    rows = FF // DP
    part = pl.BlockSpec((None, rows, count), lambda i, _: (i, 0, 0))
    shape = jax.ShapeDtypeStruct((CORES, rows, count), BF16)
    return pl.pallas_call(
        kernel,
        grid_spec=pltpu.PrefetchScalarGridSpec(
            num_scalar_prefetch=1,
            grid=(CORES,),
            in_specs=[
                pl.BlockSpec((rows, T), lambda i, order_ref: (order_ref[i], 0)),
                pl.BlockSpec((rows, T), lambda i, order_ref: (order_ref[CORES + i], 0)),
                pl.BlockSpec((T, count), lambda *_: (0, first // count), pipeline_mode=pl.Buffered(1)),
                *(ANY,) * n_after,
            ],
            out_specs=[part, part],
        ),
        out_shape=[shape, shape],
        compiler_params=params(),
        cost_estimate=cost(count / D, 20e6),
    )(order, act_t, act_t, by_out, *after)


def into_states(dg, du, w_gate, w_up, h, by_out, after):
    tile = 256
    n_after = len(after)

    def kernel(dg_ref, du_ref, wg_ref, wu_ref, h_ref, by_ref, *rest):
        out_ref = rest[n_after]
        by_a = dot_t(dg_ref[...], wg_ref[...]).astype(BF16) + dot_t(du_ref[...], wu_ref[...]).astype(BF16)
        c, wide = by_a.astype(F32), h_ref[...].astype(F32)
        scale = root_mean_scale(wide)
        along = jnp.sum(c * wide, -1, keepdims=True)
        out_ref[...] = by_ref[...] + (c * scale - wide * (scale * scale * scale * along * (1.0 / D))).astype(BF16)

    long = pl.BlockSpec((tile, FF), lambda i: (i, 0))
    short = pl.BlockSpec((tile, D), lambda i: (i, 0))
    weight = pl.BlockSpec((None, D, FF), lambda i: (1, 0, 0), pipeline_mode=pl.Buffered(1))
    return pl.pallas_call(
        kernel,
        grid=(T // tile,),
        in_specs=[long, long, weight, weight, short, short, *(ANY,) * n_after],
        out_specs=short,
        out_shape=jax.ShapeDtypeStruct((T, D), BF16),
        compiler_params=params(),
        cost_estimate=cost(2, 50e6),
    )(dg, du, w_gate, w_up, h, by_out, *after)


def solution(mesh):
    sibling = [(i, i ^ 1) for i in range(DP)]
    across = [(i, i ^ 2) for i in range(DP)]

    def step(x, dy, w_gate, w_up, w_down, m_gate, m_up, m_down, v_gate, v_up, v_down):
        x, dy = x[0], dy[0]
        me = lax.axis_index("dp")
        chip, core = me // CORES, me % CORES
        far, near = (1 - chip) * CORES, chip * CORES
        order = jnp.stack([far + 1 - core, near + 1 - core, far + core, near + core]).astype(jnp.int32)
        weights = (w_gate, w_up, w_down)

        def meet(send, keep, axis):
            got = lax.ppermute(send, "dp", sibling)
            pick = functools.partial(lax.index_in_dim, axis=axis, keepdims=False)
            there = (pick(keep, 0).astype(F32) + pick(got, 0).astype(F32)).astype(BF16)
            landed = lax.ppermute(there, "dp", across)
            return there, (pick(keep, 1), pick(got, 1), landed)

        def total(terms):
            one, two, three = (t.astype(F32) for t in terms)
            return (one + two + three).astype(BF16)

        g1, u1, a1, h1, a2 = forward_first(x, *weights)
        units, after, chain = {}, (), ()
        for name, first, count in (("b0", 0, 3), ("b1", 3, 4), ("b2", 7, 4)):
            send, keep, *chain = hidden(1, first, count, order, a2, dy, weights, None, chain, after)
            there, units[name] = meet(send, keep, 1)
            after = (there,)
        act2, dg2, du2 = chain
        send, keep = down_grad(order, act2, dy, 0, D, after)
        there, units["d2"] = meet(send, keep, 0)
        dh1 = into_states(dg2, du2, w_gate, w_up, h1, dy, (send,))
        after, chain = (there,), ()
        for name, first, count in (("e0", 0, 5), ("e1", 5, 6)):
            send, keep, *chain = hidden(0, first, count, order, a1, dh1, weights, (g1, u1), chain, after)
            there, units[name] = meet(send, keep, 1)
            after = (there,)
        (act1,) = chain
        for name, first in (("f0", 0), ("f1", D // 2)):
            send, keep = down_grad(order, act1, dh1, first, D // 2, after)
            there, units[name] = meet(send, keep, 0)
            after = (there,)

        grads = {name: total(terms) for name, terms in units.items()}
        squares = sum(jnp.sum(g.astype(F32) ** 2) for g in grads.values())
        squares = lax.psum(squares, "dp")
        factor = jnp.minimum(1.0, 0.5 * lax.rsqrt(squares / COUNT + 1e-30))

        def joined(which):
            if which == 2:
                return jnp.stack([jnp.concatenate([grads["f0"], grads["f1"]], 1), grads["d2"]])
            first = jnp.concatenate([grads[n][which] for n in ("e0", "e1")], 1)
            second = jnp.concatenate([grads[n][which] for n in ("b0", "b1", "b2")], 1)
            return jnp.stack([first, second])

        new_w, new_m, new_v = [], [], []
        for which, (w, m, v) in enumerate(zip(weights, (m_gate, m_up, m_down), (v_gate, v_up, v_down), strict=True)):
            rows = w.shape[1] // DP
            full = jnp.zeros(w.shape, BF16)
            g = joined(which).astype(F32) * factor
            m = 0.9 * m + 0.1 * g
            v = 0.95 * v + 0.05 * g * g
            own = lax.dynamic_slice_in_dim(w, me * rows, rows, 1).astype(F32)
            own = (own - 0.02 * (m * lax.rsqrt(v + 1e-8) + 0.1 * own)).astype(BF16)
            new_m.append(m)
            new_v.append(v)
            for layer in range(2):
                mine = own[layer : layer + 1]
                over = lax.ppermute(mine, "dp", across)
                beside = lax.ppermute(mine, "dp", sibling)
                corner = lax.ppermute(over, "dp", sibling)
                for piece, who in ((mine, me), (beside, me ^ 1), (over, me ^ 2), (corner, me ^ 3)):
                    full = lax.dynamic_update_slice(full, piece, (layer, who * rows, 0))
            new_w.append(full)
        return (*new_w, *new_m, *new_v)

    batch, replicated, rows = P(("rep", "dp"), None, None), P(None, None, None), P(None, "dp", None)
    return jax.shard_map(
        step,
        mesh=mesh,
        in_specs=(batch, batch, *(replicated,) * 3, *(rows,) * 6),
        out_specs=(*(P("rep", None, None),) * 3, *(P("rep", "dp", None),) * 6),
        check_vma=False,
    )
```

time: 1010 us -> 724 us (0.72)
  matrix products: 320 us -> 0 us
  Pallas kernels: 0 us -> 268 us
  waiting for transfers between devices: 502 us -> 264 us
  other arithmetic: 107 us -> 78.1 us
  local copies, waits for them, and re-layouts: 45.3 us -> 68.6 us
  starting transfers between devices: 0.37 us -> 21.9 us
  between operations: 17.6 us -> 7.46 us
    dot_general x15 -> x0, matrix products: 320 us -> none  [the longest x5 112 us: layer(): gate = jnp.dot(a, w['w_gate'], preferred_element_type=jnp.float32)]
    unnamed x15 -> x0, waiting for transfers between devices: 301 us -> none
    pallas_call x0 -> x10, Pallas kernels: none -> 268 us  [the longest x5 143 us: hidden(): pl.pallas_call(kernel, grid_spec=pltpu.PrefetchScalarGridSpec(num_scalar_...]
    ppermute x0 -> x34, waiting for transfers between devices: none -> 264 us  [the longest x8 126 us: meet(): landed = lax.ppermute(there, 'dp', across)]
    reshape x3 -> x0, waiting for transfers between devices: 201 us -> none  [step(): t.reshape(-1, *t.shape[2:])]
    unnamed x4 -> x0, other arithmetic: 48.4 us -> none
    convert_element_type x0 -> x11, other arithmetic: none -> 46.3 us  [the longest x3 29.1 us: step(): own = (own - 0.02 * (m * lax.rsqrt(v + 1e-08) + 0.1 * own)).astype(BF16)]
    unnamed x47 -> x56, local copies, waits for them, and re-layouts: 44.7 us -> 3.93 us
  transfers between devices with their start and end apart: 9 -> 34, of which waited for: 7 -> 17; matrix products, arithmetic and copies ran while one was open for 28% -> 14% of each run, Pallas kernels for 0% -> 8%
where the time goes in v1:
time: 724 us; the launch traced here: 715 us
  Pallas kernels  268 us (37%)
  waiting for transfers between devices  264 us (36%)
  other arithmetic  78.1 us (11%)
  local copies, waits for them, and re-layouts  68.6 us (9%)
  starting transfers between devices  21.9 us (3%)
  between operations  7.46 us (1%)
    pallas_call x5, Pallas kernels, hidden(): pl.pallas_call(kernel, grid_spec=pltpu.PrefetchScalarGridSpec(num_scalar_...  143 us
    ppermute x8, waiting for transfers between devices, meet(): landed = lax.ppermute(there, 'dp', across)  126 us
    ppermute x6, waiting for transfers between devices, step(): over = lax.ppermute(mine, 'dp', across)  123 us
    pallas_call x1, Pallas kernels, forward_first(): pl.pallas_call(kernel, grid=(CHUNKS,), in_specs=[whole((T, D)), pl.BlockS...  50.7 us
    pallas_call x3, Pallas kernels, down_grad(): pl.pallas_call(kernel, grid_spec=pltpu.PrefetchScalarGridSpec(num_scalar_...  40.5 us
    pallas_call x1, Pallas kernels, into_states(): pl.pallas_call(kernel, grid=(T // tile,), in_specs=[long, long, weight, w...  33.8 us
    dynamic_update_slice x21, local copies, waits for them, and re-layouts, step(): full = lax.dynamic_update_slice(full, piece, (layer, who * rows, 0))  29.9 us
    convert_element_type x3, other arithmetic, step(): own = (own - 0.02 * (m * lax.rsqrt(v + 1e-08) + 0.1 * own)).astype(BF16)  29.1 us
  transfers between devices with their start and end apart: 34, of which 17 were waited for; matrix products, arithmetic and copies ran while one was open for 14% of the time, Pallas kernels for 8%

profile of v1, /device:TPU:0, one launch (start us, length us, event | category | flops | bytes accessed | tf_op | source)
XLA Modules:
  0.0 714.6 jit_solution(14196790722416747370)
XLA Ops:
  1.3 50.7 %shard_map.178 = (f32[2048,2816]{1,0:T(8,128)}, f32[2048,2816]{1,0:T(8,128)}, bf16[2048,1024]{1,0:T(8,128)(2,1)}, bf16[2048,1024]{1,0:T(8,128)(2,1)}, bf16[2048,1024]{1,0:T(8,128)(2,1)}) custom-call(bf16[2048,1024]{1,0:T(8,128)(2,1)} %bitcast.97, bf16[2,1024,2816]{2,1,0:T(8,128)(2,1)} %wg_ref.3, bf16[2,1024,2816]{2,1,0:T(8,128)(2,1)} %wu_ref.3, ...), custom_call_target="tpu_custom_call" | custom-call | flops 35433480192 | bytes 90000000 | tf_op jit(solution)/shard_map/pallas_call | solution.py:79
  51.9 24.8 %shard_map.179 = (bf16[2,2,256,768]{3,2,1,0:T(8,128)(2,1)}, bf16[2,2,256,768]{3,2,1,0:T(8,128)(2,1)}, bf16[2816,2048]{1,0:T(8,128)(2,1)}, bf16[2048,2816]{1,0:T(8,128)(2,1)}, bf16[2048,2816]{1,0:T(8,128)(2,1)}) custom-call(s32[4]{0:T(128)} %pad_add_fusion.order_ref, bf16[2048,1024]{1,0:T(8,128)(2,1)} %get-tuple-element.42.n_ref, ...), custom_call_target="tpu_custom_call" | custom-call | flops 16106127360 | bytes 16363636 | tf_op jit(solution)/shard_map/pallas_call | solution.py:150
  83.7 30.4 %shard_map.180 = (bf16[2,2,256,1024]{3,2,1,0:T(8,128)(2,1)}, bf16[2,2,256,1024]{3,2,1,0:T(8,128)(2,1)}, bf16[2816,2048]{1,0:T(8,128)(2,1)}, bf16[2048,2816]{1,0:T(8,128)(2,1)}, bf16[2048,2816]{1,0:T(8,128)(2,1)}) custom-call(s32[4]{0:T(128)} %pad_add_fusion.order_ref, ...), custom_call_target="tpu_custom_call", output_to_operand_aliasing={{2}: (6, {}), {3}: (7, {}), {4}: (8, {})} | custom-call | flops 21474836480 | bytes 21818180 | tf_op jit(solution)/shard_map/pallas_call | solution.py:150
  121.9 30.8 %shard_map.181 = (bf16[2,2,256,1024]{3,2,1,0:T(8,128)(2,1)}, bf16[2,2,256,1024]{3,2,1,0:T(8,128)(2,1)}, bf16[2816,2048]{1,0:T(8,128)(2,1)}, bf16[2048,2816]{1,0:T(8,128)(2,1)}, bf16[2048,2816]{1,0:T(8,128)(2,1)}) custom-call(s32[4]{0:T(128)} %pad_add_fusion.order_ref, ...), custom_call_target="tpu_custom_call", output_to_operand_aliasing={{2}: (6, {}), {3}: (7, {}), {4}: (8, {})} | custom-call | flops 21474836480 | bytes 21818180 | tf_op jit(solution)/shard_map/pallas_call | solution.py:150
  160.5 18.0 %shard_map.182 = (bf16[2,704,1024]{2,1,0:T(8,128)(2,1)}, bf16[2,704,1024]{2,1,0:T(8,128)(2,1)}) custom-call(s32[4]{0:T(128)} %pad_add_fusion.order_ref, bf16[2816,2048]{1,0:T(8,128)(2,1)} %get-tuple-element.56.send_act.keep_act, bf16[2816,2048]{1,0:T(8,128)(2,1)} %get-tuple-element.56.send_act.keep_act, bf16[2048,1024]{1,0:T(8,128)(2,1)} %bitcast.101, ...), custom_call_target="tpu_custom_call" | custom-call | flops 11811160064 | bytes 20000000 | tf_op jit(solution)/shard_map/pallas_call | solution.py:183
  178.8 33.8 %shard_map.183.by_ref = bf16[2048,1024]{1,0:T(8,128)(2,1)} custom-call(bf16[2048,2816]{1,0:T(8,128)(2,1)} %get-tuple-element.53.dg_ref, bf16[2048,2816]{1,0:T(8,128)(2,1)} %get-tuple-element.54.du_ref, bf16[2,1024,2816]{2,1,0:T(8,128)(2,1)} %wg_ref.3, bf16[2,1024,2816]{2,1,0:T(8,128)(2,1)} %wu_ref.3, bf16[2048,1024]{1,0:T(8,128)(2,1)} %get-tuple-element.55.h_ref, ...), custom_call_target="tpu_custom_call" | custom-call | flops 23622320128 | bytes 50000000 | tf_op jit(solution)/shard_map/pallas_call | solution.py:217
  216.1 26.8 %shard_map.184 = (bf16[2,2,256,1280]{3,2,1,0:T(8,128)(2,1)}, bf16[2,2,256,1280]{3,2,1,0:T(8,128)(2,1)}, bf16[2816,2048]{1,0:T(8,128)(2,1)}) custom-call(s32[4]{0:T(128)} %pad_add_fusion.order_ref, bf16[2048,1024]{1,0:T(8,128)(2,1)} %get-tuple-element.41.n_ref, bf16[2048,1024]{1,0:T(8,128)(2,1)} %shard_map.183.by_ref, bf16[2,2816,1024]{2,1,0:T(8,128)(2,1)} %wd_ref.11, ...), custom_call_target="tpu_custom_call" | custom-call | flops 16106127360 | bytes 27272728 | tf_op jit(solution)/shard_map/pallas_call | solution.py:150
  251.9 30.3 %shard_map.185 = (bf16[2,2,256,1536]{3,2,1,0:T(8,128)(2,1)}, bf16[2,2,256,1536]{3,2,1,0:T(8,128)(2,1)}, bf16[2816,2048]{1,0:T(8,128)(2,1)}) custom-call(s32[4]{0:T(128)} %pad_add_fusion.order_ref, bf16[2048,1024]{1,0:T(8,128)(2,1)} %get-tuple-element.41.n_ref, bf16[2048,1024]{1,0:T(8,128)(2,1)} %shard_map.183.by_ref, ...), custom_call_target="tpu_custom_call", output_to_operand_aliasing={{2}: (6, {})} | custom-call | flops 19327352832 | bytes 32727272 | tf_op jit(solution)/shard_map/pallas_call | solution.py:150
  287.3 18.2 %collective-permute-done.8 = bf16[2,256,768]{2,1,0:T(8,128)(2,1)} collective-permute-done((bf16[2,256,768]{2,1,0:T(8,128)(2,1)}, bf16[2,256,768]{2,1,0:T(8,128)(2,1)}, u32[]{:S(2)}, u32[]{:S(2)}) %collective-permute-start.8) | collective-permute-done | bytes 786464 | tf_op jit(solution)/shard_map/ppermute | solution.py:244
  313.9 11.2 %shard_map.186 = (bf16[2,704,512]{2,1,0:T(8,128)(2,1)}, bf16[2,704,512]{2,1,0:T(8,128)(2,1)}) custom-call(s32[4]{0:T(128)} %pad_add_fusion.order_ref, bf16[2816,2048]{1,0:T(8,128)(2,1)} %get-tuple-element.68.send_act.keep_act, bf16[2816,2048]{1,0:T(8,128)(2,1)} %get-tuple-element.68.send_act.keep_act, bf16[2048,1024]{1,0:T(8,128)(2,1)} %shard_map.183.by_ref, ...), custom_call_target="tpu_custom_call" | custom-call | flops 5905580032 | bytes 20000000 | tf_op jit(solution)/shard_map/pallas_call | solution.py:183
  325.1 10.2 %collective-permute-done.9 = bf16[2,256,1024]{2,1,0:T(8,128)(2,1)} collective-permute-done((bf16[2,256,1024]{2,1,0:T(8,128)(2,1)}, bf16[2,256,1024]{2,1,0:T(8,128)(2,1)}, u32[]{:S(2)}, u32[]{:S(2)}) %collective-permute-start.9) | collective-permute-done | bytes 1048608 | tf_op jit(solution)/shard_map/ppermute | solution.py:244
  339.8 16.5 %collective-permute-done.10 = bf16[2,256,1024]{2,1,0:T(8,128)(2,1)} collective-permute-done((bf16[2,256,1024]{2,1,0:T(8,128)(2,1)}, bf16[2,256,1024]{2,1,0:T(8,128)(2,1)}, u32[]{:S(2)}, u32[]{:S(2)}) %collective-permute-start.10) | collective-permute-done | bytes 1048608 | tf_op jit(solution)/shard_map/ppermute | solution.py:244
  367.6 11.4 %shard_map.187 = (bf16[2,704,512]{2,1,0:T(8,128)(2,1)}, bf16[2,704,512]{2,1,0:T(8,128)(2,1)}) custom-call(s32[4]{0:T(128)} %pad_add_fusion.order_ref, bf16[2816,2048]{1,0:T(8,128)(2,1)} %get-tuple-element.68.send_act.keep_act, bf16[2816,2048]{1,0:T(8,128)(2,1)} %get-tuple-element.68.send_act.keep_act, bf16[2048,1024]{1,0:T(8,128)(2,1)} %shard_map.183.by_ref, ...), custom_call_target="tpu_custom_call" | custom-call | flops 5905580032 | bytes 20000000 | tf_op jit(solution)/shard_map/pallas_call | solution.py:183
  379.0 14.9 %collective-permute-done.11 = bf16[704,1024]{1,0:T(8,128)(2,1)} collective-permute-done((bf16[704,1024]{1,0:T(8,128)(2,1)}, bf16[704,1024]{1,0:T(8,128)(2,1)}, u32[]{:S(2)}, u32[]{:S(2)}) %collective-permute-start.11) | collective-permute-done | bytes 1441824 | tf_op jit(solution)/shard_map/ppermute | solution.py:244
  399.5 22.5 %collective-permute-done.5 = bf16[2,256,1280]{2,1,0:T(8,128)(2,1)} collective-permute-done((bf16[2,256,1280]{2,1,0:T(8,128)(2,1)}, bf16[2,256,1280]{2,1,0:T(8,128)(2,1)}, u32[]{:S(2)}, u32[]{:S(2)}) %collective-permute-start.5) | collective-permute-done | bytes 1310752 | tf_op jit(solution)/shard_map/ppermute | solution.py:244
  428.6 27.1 %collective-permute-done.7 = bf16[2,256,1536]{2,1,0:T(8,128)(2,1)} collective-permute-done((bf16[2,256,1536]{2,1,0:T(8,128)(2,1)S(1)}, bf16[2,256,1536]{2,1,0:T(8,128)(2,1)}, u32[]{:S(2)}, u32[]{:S(2)}) %collective-permute-start.7) | collective-permute-done | bytes 1572896 | tf_op jit(solution)/shard_map/ppermute | solution.py:244
  496.9 10.1 %fusion.2 = (bf16[2,256,2816]{2,1,0:T(8,128)(2,1)S(1)}, f32[2,256,2816]{2,1,0:T(8,128)}, f32[2,256,2816]{2,1,0:T(8,128)}) fusion(bf16[2,1024,2816]{2,1,0:T(8,128)(2,1)} %wg_ref.3, s32[]{:T(128)S(6)} %select_n.27, f32[]{:T(128)S(6)} %min_shard_map.3, bf16[1,256,2816]{2,1,0:T(8,128)(2,1)} %get-tuple-element.117, bf16[1,256,2816]{2,1,0:T(8,128)(2,1)} %get-tuple-element.119, ...), kind=kLoop, calls=%fused_computation.11 | loop fusion | flops 28835840 | bytes 31719432 | tf_op jit(solution)/shard_map/convert_element_type | solution.py:292
  515.9 9.4 %fusion.8 = (bf16[2,704,1024]{2,1,0:T(8,128)(2,1)S(1)}, f32[2,704,1024]{2,1,0:T(8,128)}, f32[2,704,1024]{2,1,0:T(8,128)}) fusion(bf16[2,2816,1024]{2,1,0:T(8,128)(2,1)} %wd_ref.11, s32[]{:T(128)S(6)} %select_n.60, f32[]{:T(128)S(6)} %min_shard_map.3, bf16[1,704,1024]{2,1,0:T(8,128)(2,1)S(1)} %copy-done.8, ...), kind=kLoop, calls=%fused_computation.17 | loop fusion | flops 28835840 | bytes 31719432 | tf_op jit(solution)/shard_map/convert_element_type | solution.py:292
  534.4 9.5 %fusion.5 = (bf16[2,256,2816]{2,1,0:T(8,128)(2,1)S(1)}, f32[2,256,2816]{2,1,0:T(8,128)}, f32[2,256,2816]{2,1,0:T(8,128)}) fusion(bf16[2,1024,2816]{2,1,0:T(8,128)(2,1)} %wu_ref.3, s32[]{:T(128)S(6)} %select_n.27, f32[]{:T(128)S(6)} %min_shard_map.3, bf16[1,256,2816]{2,1,0:T(8,128)(2,1)S(1)} %copy-done.7, bf16[1,256,2816]{2,1,0:T(8,128)(2,1)S(1)} %copy-done.9, ...), kind=kLoop, calls=%fused_computation.14 | loop fusion | flops 28835840 | bytes 31719432 | tf_op jit(solution)/shard_map/convert_element_type | solution.py:292
  552.9 27.3 %collective-permute-done.29 = bf16[1,704,1024]{2,1,0:T(8,128)(2,1)} collective-permute-done((bf16[1,704,1024]{2,1,0:T(8,128)(2,1)S(1)}, bf16[1,704,1024]{2,1,0:T(8,128)(2,1)}, u32[]{:S(2)}, u32[]{:S(2)}) %collective-permute-start.29) | collective-permute-done | bytes 1441824 | tf_op jit(solution)/shard_map/ppermute | solution.py:297
  594.4 16.7 %collective-permute-done.23 = bf16[1,256,2816]{2,1,0:T(8,128)(2,1)} collective-permute-done((bf16[1,256,2816]{2,1,0:T(8,128)(2,1)}, bf16[1,256,2816]{2,1,0:T(8,128)(2,1)}, u32[]{:S(2)}, u32[]{:S(2)}) %collective-permute-start.23) | collective-permute-done | bytes 1441824 | tf_op jit(solution)/shard_map/ppermute | solution.py:297
  621.1 20.8 %collective-permute-done.32 = bf16[1,704,1024]{2,1,0:T(8,128)(2,1)S(1)} collective-permute-done((bf16[1,704,1024]{2,1,0:T(8,128)(2,1)}, bf16[1,704,1024]{2,1,0:T(8,128)(2,1)S(1)}, u32[]{:S(2)}, u32[]{:S(2)}) %collective-permute-start.32) | collective-permute-done | bytes 1441824 | tf_op jit(solution)/shard_map/ppermute | solution.py:297
  644.8 28.0 %collective-permute-done.20 = bf16[1,256,2816]{2,1,0:T(8,128)(2,1)S(1)} collective-permute-done((bf16[1,256,2816]{2,1,0:T(8,128)(2,1)S(1)}, bf16[1,256,2816]{2,1,0:T(8,128)(2,1)S(1)}, u32[]{:S(2)}, u32[]{:S(2)}) %collective-permute-start.20) | collective-permute-done | bytes 1441824 | tf_op jit(solution)/shard_map/ppermute | solution.py:297
  672.8 30.4 %collective-permute-done.26 = bf16[1,256,2816]{2,1,0:T(8,128)(2,1)S(1)} collective-permute-done((bf16[1,256,2816]{2,1,0:T(8,128)(2,1)S(1)}, bf16[1,256,2816]{2,1,0:T(8,128)(2,1)S(1)}, u32[]{:S(2)}, u32[]{:S(2)}) %collective-permute-start.26) | collective-permute-done | bytes 1441824 | tf_op jit(solution)/shard_map/ppermute | solution.py:297
  (171 shorter events, 177.3 us)
Async XLA Ops:
  178.4 34.2 %collective-permute-start.3 = (bf16[2,704,1024]{2,1,0:T(8,128)(2,1)}, bf16[2,704,1024]{2,1,0:T(8,128)(2,1)}, u32[]{:S(2)}, u32[]{:S(2)}) collective-permute-start(bf16[2,704,1024]{2,1,0:T(8,128)(2,1)} %get-tuple-element.59.rest_0_), channel_id=1, source_target_pairs={{0,1},{1,0},{2,3},{3,2},{4,5},{5,4},{6,7},{7,6}} | collective-permute-start | bytes 8650760 | tf_op jit(solution)/shard_map/ppermute | solution.py:241
  284.3 26.7 %collective-permute-start.6 = (bf16[2,2,256,1536]{3,2,0,1:T(8,128)(2,1)S(1)}, bf16[2,2,256,1536]{3,2,0,1:T(8,128)(2,1)}, u32[]{:S(2)}, u32[]{:S(2)}) collective-permute-start(bf16[2,2,256,1536]{3,2,0,1:T(8,128)(2,1)S(1)} %copy.37), channel_id=1, source_target_pairs={{0,1},{1,0},{2,3},{3,2},{4,5},{5,4},{6,7},{7,6}} | collective-permute-start | bytes 9437192 | tf_op jit(solution)/shard_map/ppermute | solution.py:241
  310.7 45.7 %collective-permute-start.10 = (bf16[2,256,1024]{2,1,0:T(8,128)(2,1)}, bf16[2,256,1024]{2,1,0:T(8,128)(2,1)}, u32[]{:S(2)}, u32[]{:S(2)}) collective-permute-start(bf16[2,256,1024]{2,1,0:T(8,128)(2,1)} %fusion.24.rest_0_), channel_id=1, source_target_pairs={{0,2},{1,3},{2,0},{3,1},{4,6},{5,7},{6,4},{7,5}} | collective-permute-start | bytes 3145736 | tf_op jit(solution)/shard_map/ppermute | solution.py:244
  325.1 40.3 %collective-permute-start.12 = (bf16[2,704,512]{2,1,0:T(8,128)(2,1)}, bf16[2,704,512]{2,1,0:T(8,128)(2,1)}, u32[]{:S(2)}, u32[]{:S(2)}) collective-permute-start(bf16[2,704,512]{2,1,0:T(8,128)(2,1)} %get-tuple-element.70), channel_id=1, source_target_pairs={{0,1},{1,0},{2,3},{3,2},{4,5},{5,4},{6,7},{7,6}} | collective-permute-start | bytes 4325384 | tf_op jit(solution)/shard_map/ppermute | solution.py:241
  359.1 34.8 %collective-permute-start.11 = (bf16[704,1024]{1,0:T(8,128)(2,1)}, bf16[704,1024]{1,0:T(8,128)(2,1)}, u32[]{:S(2)}, u32[]{:S(2)}) collective-permute-start(bf16[704,1024]{1,0:T(8,128)(2,1)} %fusion.19.rest_0_), channel_id=1, source_target_pairs={{0,2},{1,3},{2,0},{3,1},{4,6},{5,7},{6,4},{7,5}} | collective-permute-start | bytes 4325384 | tf_op jit(solution)/shard_map/ppermute | solution.py:244
  360.7 61.3 %collective-permute-start.5 = (bf16[2,256,1280]{2,1,0:T(8,128)(2,1)}, bf16[2,256,1280]{2,1,0:T(8,128)(2,1)}, u32[]{:S(2)}, u32[]{:S(2)}) collective-permute-start(bf16[2,256,1280]{2,1,0:T(8,128)(2,1)} %fusion.22.rest_1_), channel_id=1, source_target_pairs={{0,2},{1,3},{2,0},{3,1},{4,6},{5,7},{6,4},{7,5}} | collective-permute-start | bytes 3932168 | tf_op jit(solution)/shard_map/ppermute | solution.py:244
  363.9 91.8 %collective-permute-start.7 = (bf16[2,256,1536]{2,1,0:T(8,128)(2,1)S(1)}, bf16[2,256,1536]{2,1,0:T(8,128)(2,1)}, u32[]{:S(2)}, u32[]{:S(2)}) collective-permute-start(bf16[2,256,1536]{2,1,0:T(8,128)(2,1)S(1)} %copy-done.6), channel_id=1, source_target_pairs={{0,2},{1,3},{2,0},{3,1},{4,6},{5,7},{6,4},{7,5}} | collective-permute-start | bytes 4718600 | tf_op jit(solution)/shard_map/ppermute | solution.py:244
  379.0 81.2 %collective-permute-start.14 = (bf16[2,704,512]{2,1,0:T(8,128)(2,1)}, bf16[2,704,512]{2,1,0:T(8,128)(2,1)}, u32[]{:S(2)}, u32[]{:S(2)}) collective-permute-start(bf16[2,704,512]{2,1,0:T(8,128)(2,1)} %get-tuple-element.72), channel_id=1, source_target_pairs={{0,1},{1,0},{2,3},{3,2},{4,5},{5,4},{6,7},{7,6}} | collective-permute-start | bytes 4325384 | tf_op jit(solution)/shard_map/ppermute | solution.py:241
  427.2 44.0 %collective-permute-start.13 = (bf16[704,512]{1,0:T(8,128)(2,1)}, bf16[704,512]{1,0:T(8,128)(2,1)}, u32[]{:S(2)}, u32[]{:S(2)}) collective-permute-start(bf16[704,512]{1,0:T(8,128)(2,1)} %fusion.26.rest_0_), channel_id=1, source_target_pairs={{0,2},{1,3},{2,0},{3,1},{4,6},{5,7},{6,4},{7,5}} | collective-permute-start | bytes 2162696 | tf_op jit(solution)/shard_map/ppermute | solution.py:244
  514.5 37.2 %collective-permute-start.16 = (bf16[1,256,2816]{2,1,0:T(8,128)(2,1)}, bf16[1,256,2816]{2,1,0:T(8,128)(2,1)}, u32[]{:S(2)}, u32[]{:S(2)}) collective-permute-start(bf16[1,256,2816]{2,1,0:T(8,128)(2,1)} %get-tuple-element.106), channel_id=1, source_target_pairs={{0,1},{1,0},{2,3},{3,2},{4,5},{5,4},{6,7},{7,6}} | collective-permute-start | bytes 4325384 | tf_op jit(solution)/shard_map/ppermute | solution.py:298
  514.5 71.7 %collective-permute-start.17 = (bf16[1,256,2816]{2,1,0:T(8,128)(2,1)}, bf16[1,256,2816]{2,1,0:T(8,128)(2,1)}, u32[]{:S(2)}, u32[]{:S(2)}) collective-permute-start(bf16[1,256,2816]{2,1,0:T(8,128)(2,1)} %get-tuple-element.106), channel_id=1, source_target_pairs={{0,2},{1,3},{2,0},{3,1},{4,6},{5,7},{6,4},{7,5}} | collective-permute-start | bytes 4325384 | tf_op jit(solution)/shard_map/ppermute | solution.py:297
  533.5 46.7 %collective-permute-start.29 = (bf16[1,704,1024]{2,1,0:T(8,128)(2,1)S(1)}, bf16[1,704,1024]{2,1,0:T(8,128)(2,1)}, u32[]{:S(2)}, u32[]{:S(2)}) collective-permute-start(bf16[1,704,1024]{2,1,0:T(8,128)(2,1)S(1)} %get-tuple-element.100), channel_id=1, source_target_pairs={{0,2},{1,3},{2,0},{3,1},{4,6},{5,7},{6,4},{7,5}} | collective-permute-start | bytes 4325384 | tf_op jit(solution)/shard_map/ppermute | solution.py:297
  551.5 41.2 %collective-permute-start.22 = (bf16[1,256,2816]{2,1,0:T(8,128)(2,1)}, bf16[1,256,2816]{2,1,0:T(8,128)(2,1)}, u32[]{:S(2)}, u32[]{:S(2)}) collective-permute-start(bf16[1,256,2816]{2,1,0:T(8,128)(2,1)} %get-tuple-element.103), channel_id=1, source_target_pairs={{0,1},{1,0},{2,3},{3,2},{4,5},{5,4},{6,7},{7,6}} | collective-permute-start | bytes 4325384 | tf_op jit(solution)/shard_map/ppermute | solution.py:298
  551.8 59.3 %collective-permute-start.23 = (bf16[1,256,2816]{2,1,0:T(8,128)(2,1)}, bf16[1,256,2816]{2,1,0:T(8,128)(2,1)}, u32[]{:S(2)}, u32[]{:S(2)}) collective-permute-start(bf16[1,256,2816]{2,1,0:T(8,128)(2,1)} %get-tuple-element.103), channel_id=1, source_target_pairs={{0,2},{1,3},{2,0},{3,1},{4,6},{5,7},{6,4},{7,5}} | collective-permute-start | bytes 4325384 | tf_op jit(solution)/shard_map/ppermute | solution.py:297
  552.7 59.6 %collective-permute-start.31 = (bf16[1,704,1024]{2,1,0:T(8,128)(2,1)}, bf16[1,704,1024]{2,1,0:T(8,128)(2,1)}, u32[]{:S(2)}, u32[]{:S(2)}) collective-permute-start(bf16[1,704,1024]{2,1,0:T(8,128)(2,1)} %get-tuple-element.98), channel_id=1, source_target_pairs={{0,1},{1,0},{2,3},{3,2},{4,5},{5,4},{6,7},{7,6}} | collective-permute-start | bytes 4325384 | tf_op jit(solution)/shard_map/ppermute | solution.py:298
  580.2 33.0 %collective-permute-start.30 = (bf16[1,704,1024]{2,1,0:T(8,128)(2,1)}, bf16[1,704,1024]{2,1,0:T(8,128)(2,1)}, u32[]{:S(2)}, u32[]{:S(2)}) collective-permute-start(bf16[1,704,1024]{2,1,0:T(8,128)(2,1)} %collective-permute-done.29), channel_id=1, source_target_pairs={{0,1},{1,0},{2,3},{3,2},{4,5},{5,4},{6,7},{7,6}} | collective-permute-start | bytes 4325384 | tf_op jit(solution)/shard_map/ppermute | solution.py:299
  586.2 55.7 %collective-permute-start.32 = (bf16[1,704,1024]{2,1,0:T(8,128)(2,1)}, bf16[1,704,1024]{2,1,0:T(8,128)(2,1)S(1)}, u32[]{:S(2)}, u32[]{:S(2)}) collective-permute-start(bf16[1,704,1024]{2,1,0:T(8,128)(2,1)} %get-tuple-element.98), channel_id=1, source_target_pairs={{0,2},{1,3},{2,0},{3,1},{4,6},{5,7},{6,4},{7,5}} | collective-permute-start | bytes 4325384 | tf_op jit(solution)/shard_map/ppermute | solution.py:297
  592.7 50.4 %collective-permute-start.18 = (bf16[1,256,2816]{2,1,0:T(8,128)(2,1)}, bf16[1,256,2816]{2,1,0:T(8,128)(2,1)S(1)}, u32[]{:S(2)}, u32[]{:S(2)}) collective-permute-start(bf16[1,256,2816]{2,1,0:T(8,128)(2,1)} %collective-permute-done.17), channel_id=1, source_target_pairs={{0,1},{1,0},{2,3},{3,2},{4,5},{5,4},{6,7},{7,6}} | collective-permute-start | bytes 4325384 | tf_op jit(solution)/shard_map/ppermute | solution.py:299
  611.1 61.7 %collective-permute-start.20 = (bf16[1,256,2816]{2,1,0:T(8,128)(2,1)S(1)}, bf16[1,256,2816]{2,1,0:T(8,128)(2,1)S(1)}, u32[]{:S(2)}, u32[]{:S(2)}) collective-permute-start(bf16[1,256,2816]{2,1,0:T(8,128)(2,1)S(1)} %copy-done.25), channel_id=1, source_target_pairs={{0,2},{1,3},{2,0},{3,1},{4,6},{5,7},{6,4},{7,5}} | collective-permute-start | bytes 4325384 | tf_op jit(solution)/shard_map/ppermute | solution.py:297
  612.3 90.9 %collective-permute-start.26 = (bf16[1,256,2816]{2,1,0:T(8,128)(2,1)S(1)}, bf16[1,256,2816]{2,1,0:T(8,128)(2,1)S(1)}, u32[]{:S(2)}, u32[]{:S(2)}) collective-permute-start(bf16[1,256,2816]{2,1,0:T(8,128)(2,1)S(1)} %copy-done.26), channel_id=1, source_target_pairs={{0,2},{1,3},{2,0},{3,1},{4,6},{5,7},{6,4},{7,5}} | collective-permute-start | bytes 4325384 | tf_op jit(solution)/shard_map/ppermute | solution.py:297
  613.2 90.1 %collective-permute-start.24 = (bf16[1,256,2816]{2,1,0:T(8,128)(2,1)}, bf16[1,256,2816]{2,1,0:T(8,128)(2,1)S(1)}, u32[]{:S(2)}, u32[]{:S(2)}) collective-permute-start(bf16[1,256,2816]{2,1,0:T(8,128)(2,1)} %collective-permute-done.23), channel_id=1, source_target_pairs={{0,1},{1,0},{2,3},{3,2},{4,5},{5,4},{6,7},{7,6}} | collective-permute-start | bytes 4325384 | tf_op jit(solution)/shard_map/ppermute | solution.py:299
  641.9 63.3 %collective-permute-start.19 = (bf16[1,256,2816]{2,1,0:T(8,128)(2,1)S(1)}, bf16[1,256,2816]{2,1,0:T(8,128)(2,1)S(1)}, u32[]{:S(2)}, u32[]{:S(2)}) collective-permute-start(bf16[1,256,2816]{2,1,0:T(8,128)(2,1)S(1)} %copy-done.25), channel_id=1, source_target_pairs={{0,1},{1,0},{2,3},{3,2},{4,5},{5,4},{6,7},{7,6}} | collective-permute-start | bytes 4325384 | tf_op jit(solution)/shard_map/ppermute | solution.py:298
  643.1 64.5 %collective-permute-start.25 = (bf16[1,256,2816]{2,1,0:T(8,128)(2,1)S(1)}, bf16[1,256,2816]{2,1,0:T(8,128)(2,1)S(1)}, u32[]{:S(2)}, u32[]{:S(2)}) collective-permute-start(bf16[1,256,2816]{2,1,0:T(8,128)(2,1)S(1)} %copy-done.26), channel_id=1, source_target_pairs={{0,1},{1,0},{2,3},{3,2},{4,5},{5,4},{6,7},{7,6}} | collective-permute-start | bytes 4325384 | tf_op jit(solution)/shard_map/ppermute | solution.py:298
  672.8 36.5 %collective-permute-start.33 = (bf16[1,704,1024]{2,1,0:T(8,128)(2,1)S(1)}, bf16[1,704,1024]{2,1,0:T(8,128)(2,1)S(1)}, u32[]{:S(2)}, u32[]{:S(2)}) collective-permute-start(bf16[1,704,1024]{2,1,0:T(8,128)(2,1)S(1)} %collective-permute-done.32), channel_id=1, source_target_pairs={{0,1},{1,0},{2,3},{3,2},{4,5},{5,4},{6,7},{7,6}} | collective-permute-start | bytes 4325384 | tf_op jit(solution)/shard_map/ppermute | solution.py:299
  (38 other events, 431.7 us)
